TPU v7x, 256 devices: a whole 4x4x8 slice. The times are simulated.
256 devices in a mesh: seq: 8 (over y, x_lo), exp: 32 (over z, x_hi, core).
Axes of the slice: x: 4 (x_hi: 2, x_lo: 2; x = x_hi * 2 + x_lo), y: 4, z: 8, core: 2. Of those that a mesh axis runs over, the one named last changes fastest.
Arguments:
- tokens: bfloat16 [65536, 2048], P(('seq', 'exp')), may hold values from -128 to 128
- slot_embed: bfloat16 [2048, 256], P(None, 'exp'), may hold values from -0.397747564 to 0.397747564
- expert_in: bfloat16 [64, 2048, 4096], P('exp', None, 'seq'), may hold values from -0.125 to 0.125
- expert_out: bfloat16 [64, 4096, 2048], P('exp', 'seq'), may hold values from -0.09375 to 0.09375
- out_grad: bfloat16 [65536, 2048], P(('seq', 'exp')), may hold values from -0.59765625 to 0.59765625
Outputs:
- tok_grad: bfloat16 [65536, 2048], P(('seq', 'exp'))
- slot_grad: float32 [2048, 256], P('seq', 'exp')
All inputs are finite; a program needn't handle non-finite values.
Results may differ from a plain program's by a relative error of at most 0.024.
Values may be sent and summed in bfloat16 or wider, within the bound.
A program may use at most 64 MiB of HBM per device.

v0:
```python
from functools import partial
import functools
import jax
import jax.numpy as jnp
from jax import lax
from jax.sharding import Mesh
from jax.sharding import PartitionSpec as P

EXP = ("exp_0", "exp_1", "exp_2")
SEQ = ("seq_0", "seq_1")
SEQ_EXP = ("seq_0", "seq_1", "exp_0", "exp_1", "exp_2")


def split_up(x, dim, size):
    shape = x.shape
    blocks = x.reshape(*shape[:dim], size, shape[dim] // size, *shape[dim + 1 :])
    return jnp.moveaxis(blocks, dim, 0)


def sum_at_owner(x, axis, dim):
    size = lax.axis_size(axis)
    blocks = lax.all_to_all(split_up(x, dim, size), axis, 0, 0, tiled=True)
    return jnp.sum(blocks, axis=0)


def from_everyone(x, axis):
    copies = jnp.broadcast_to(x, (lax.axis_size(axis), *x.shape))
    return lax.all_to_all(copies, axis, split_axis=0, concat_axis=0, tiled=True)


def taken_together(x, axis):
    return from_everyone(x, axis).sum(axis=0)


def collected_together(x, axis):
    leaves = jax.tree.leaves(x)
    turns = sorted(range(len(leaves)), key=lambda k: -leaves[k].size)
    width = (1, *leaves[turns[0]].shape)[-1]
    lines = [
        jnp.pad(leaves[k].reshape(-1), (0, -leaves[k].size % width)).reshape(-1, width)
        for k in turns
    ]
    both, at, found = (lax.all_gather(jnp.concatenate(lines), axis), 0, {})
    for k, line in zip(turns, lines):
        section = both[:, at : at + len(line)].reshape(len(both), -1)
        found[k] = section[:, : leaves[k].size].reshape(-1, *leaves[k].shape)
        at += len(line)
    numbers = iter(range(len(leaves)))
    return jax.tree.map(lambda _: found[next(numbers)], x)


def joined_all(x, axes, combine):
    for axis in axes:
        pieces = collected_together(x, axis)
        x = jax.tree.map(lambda part: part[0], pieces)
        for k in range(1, lax.axis_size(axis)):
            x = combine(x, jax.tree.map(lambda part: part[k], pieces))
    return x


def one_axis_at_a_time(x, axes):
    return functools.reduce(lax.psum, axes, x)


def contract_rows(left, right):
    return lax.dot_general(
        left, right, (((0,), (0,)), ((), ())), preferred_element_type=jnp.float32
    )


def contract_cols(left, right):
    return lax.dot_general(
        left, right, (((1,), (1,)), ((), ())), preferred_element_type=jnp.float32
    )


def merge_stats(first_pair, second_pair):
    top_value = jnp.maximum(first_pair[0], second_pair[0])
    summed = first_pair[1] * jnp.exp(first_pair[0] - top_value) + second_pair[1] * jnp.exp(
        second_pair[0] - top_value
    )
    return (top_value, summed)


def owner_sum(partial_rows):
    owned = sum_at_owner(partial_rows, EXP, 0)
    return taken_together(owned, SEQ)


def shards(tokens, slot_embed, expert_in, expert_out, out_grad):
    experts_here = expert_in.shape[0]
    model_width = tokens.shape[1]
    slot_table = lax.all_gather(slot_embed, EXP, axis=1, tiled=True)
    logits = jnp.dot(tokens, slot_table, preferred_element_type=jnp.float32)
    local_top = jnp.max(logits, axis=0)
    local_total = jnp.sum(jnp.exp(logits - local_top), axis=0)
    col_top, col_total = joined_all((local_top, local_total), SEQ_EXP, merge_stats)
    dispatch = jnp.exp(logits - col_top) / col_total
    dispatch_b = dispatch.astype(jnp.bfloat16)
    combine_w = jax.nn.softmax(logits, axis=1)
    combine_b = combine_w.astype(jnp.bfloat16)
    slot_sum = owner_sum(contract_rows(dispatch_b, tokens))
    slot_in = slot_sum.astype(jnp.bfloat16).reshape(experts_here, -1, model_width)
    pre_act = jnp.einsum("esd,edh->esh", slot_in, expert_in, preferred_element_type=jnp.float32)
    hidden = jax.nn.gelu(pre_act, approximate=True).astype(jnp.bfloat16)
    out_part = jnp.einsum("esh,ehd->esd", hidden, expert_out, preferred_element_type=jnp.float32)
    slot_out = taken_together(out_part, SEQ).astype(jnp.bfloat16).reshape(-1, model_width)
    slot_all = lax.all_gather(slot_out, EXP, axis=0, tiled=True)
    comb_grad = contract_cols(out_grad, slot_all)
    grad_out = owner_sum(contract_rows(combine_b, out_grad))
    grad_out = grad_out.astype(jnp.bfloat16).reshape(experts_here, -1, model_width)
    hid_grad = jnp.einsum("esd,ehd->esh", grad_out, expert_out, preferred_element_type=jnp.float32)
    _, pullback = jax.vjp(partial(jax.nn.gelu, approximate=True), pre_act)
    act_grad = pullback(hid_grad)[0].astype(jnp.bfloat16)
    in_part = jnp.einsum("esh,edh->esd", act_grad, expert_in, preferred_element_type=jnp.float32)
    grad_own = taken_together(in_part, SEQ).astype(jnp.bfloat16).reshape(-1, model_width)
    grad_all = lax.all_gather(grad_own, EXP, axis=0, tiled=True)
    disp_grad = contract_cols(tokens, grad_all)
    centre_local = jnp.sum(dispatch_b.astype(jnp.float32) * disp_grad, axis=0)
    centre = one_axis_at_a_time(centre_local, SEQ_EXP)
    comb_mean = jnp.sum(combine_w * comb_grad, axis=1, keepdims=True)
    logit_grad = dispatch * (disp_grad - centre) + combine_w * (comb_grad - comb_mean)
    logit_b = logit_grad.astype(jnp.bfloat16)
    tok_grad = jnp.dot(dispatch_b, grad_all, preferred_element_type=jnp.float32) + contract_cols(
        logit_b, slot_table
    )
    table_part = contract_rows(tokens, logit_b)
    table_owned = sum_at_owner(table_part, EXP, 1)
    slot_grad = sum_at_owner(table_owned, SEQ, 0)
    return (tok_grad.astype(jnp.bfloat16), slot_grad)


def solution(mesh):
    torus = Mesh(mesh.devices.reshape(4, 2, 8, 2, 2), ("seq_0", "seq_1", "exp_0", "exp_1", "exp_2"))
    placed = (
        P(SEQ_EXP, None),
        P(None, EXP),
        P(EXP, None, SEQ),
        P(EXP, SEQ, None),
        P(SEQ_EXP, None),
    )
    return jax.shard_map(
        shards,
        mesh=torus,
        in_specs=placed,
        out_specs=(P(SEQ_EXP, None), P(SEQ, EXP)),
        check_vma=False,
    )
```

profile of v0, /device:TPU:4, one launch (start us, length us, event | category | flops | bytes accessed | tf_op | source)
XLA Modules:
  0.0 532.9 jit_solution(1406648568173986912)
XLA Ops:
  7.2 0.0 copy-start
  7.2 0.0 all-gather.14.cloned.1.call-start
  7.2 0.7 all-gather.14.cloned.1.call-update
  7.9 81.8 %all-gather.14.cloned.1.call-done = bf16[2048,256]{0,1:T(8,128)(2,1)} async-done(((bf16[2048,8]{0,1:T(8,128)(2,1)}), bf16[2048,256]{0,1:T(8,128)(2,1)}) %all-gather.14.cloned.1.call-update) | async-done | bytes 1048592 | tf_op jit(solution)/shard_map/all_gather | solution.py:93
  89.7 0.0 copy-done
  89.7 1.8 fusion.85
  91.5 0.2 fusion.2
  91.7 11.2 %all-gather.5 = f32[4,2,256]{2,1,0:T(2,128)S(1)} all-gather(f32[1,2,256]{2,1,0:T(2,128)S(1)} %maximum_bitcast_fusion), channel_id=2, replica_groups=mesh['seq_0'=4,'seq_1'=2,'exp_0'=8,'exp_1'=2,'exp_2'=2] {'seq_0'}, dimensions={0}, use_global_device_ids=true | all-gather | bytes 10240 | tf_op jit(solution)/shard_map/all_gather | solution.py:43
  102.9 4.4 all-gather.6
  107.3 21.6 %all-gather.7 = f32[8,2,256]{2,1,0:T(2,128)S(1)} all-gather(f32[1,2,256]{2,1,0:T(2,128)S(1)} %maximum_bitcast_fusion.2), channel_id=4, replica_groups=mesh['seq_0'=4,'seq_1'=2,'exp_0'=8,'exp_1'=2,'exp_2'=2] {'exp_0'}, dimensions={0}, use_global_device_ids=true | all-gather | bytes 18432 | tf_op jit(solution)/shard_map/all_gather | solution.py:43
  128.9 5.9 %all-gather.8 = f32[2,2,256]{2,1,0:T(2,128)S(1)} all-gather(f32[1,2,256]{2,1,0:T(2,128)S(1)} %maximum_bitcast_fusion.3), channel_id=5, replica_groups=mesh['seq_0'=4,'seq_1'=2,'exp_0'=8,'exp_1'=2,'exp_2'=2] {'exp_1'}, dimensions={0}, use_global_device_ids=true | all-gather | bytes 6144 | tf_op jit(solution)/shard_map/all_gather | solution.py:43
  134.8 1.8 all-gather.9
  136.7 1.8 convolution_bitcast_fusion.1
  138.4 7.1 %all-to-all-start.2 = ((f32[32,8,2048]{2,1,0:T(8,128)}), f32[32,8,2048]{2,1,0:T(8,128)S(1)}, u32[]{:S(2)}, u32[]{:S(2)}) async-start(f32[32,8,2048]{2,1,0:T(8,128)} %convolution_bitcast_fusion.1), calls=%async_computation.2 | async-start | bytes 4194304 | tf_op jit(solution)/shard_map/all_to_all | solution.py:22
  145.6 3.2 convolution_bitcast_fusion.2
  148.7 47.0 %all-to-all-done.2 = f32[32,8,2048]{2,1,0:T(8,128)S(1)} async-done(((f32[32,8,2048]{2,1,0:T(8,128)}), f32[32,8,2048]{2,1,0:T(8,128)S(1)}, u32[]{:S(2)}, u32[]{:S(2)}) %all-to-all-start.2) | async-done | bytes 2097184 | tf_op jit(solution)/shard_map/all_to_all | solution.py:22
  195.7 1.3 copy-done.1
  197.0 6.3 %all-to-all-start = ((f32[32,8,2048]{2,1,0:T(8,128)}), f32[32,8,2048]{2,1,0:T(8,128)S(1)}, u32[]{:S(2)}, u32[]{:S(2)}) async-start(f32[32,8,2048]{2,1,0:T(8,128)} %convolution_bitcast_fusion.2), calls=%async_computation | async-start | bytes 4194304 | tf_op jit(solution)/shard_map/all_to_all | solution.py:22
  203.3 1.7 reduce_sum.112
  205.0 48.5 %all-to-all-done = f32[32,8,2048]{2,1,0:T(8,128)S(1)} async-done(((f32[32,8,2048]{2,1,0:T(8,128)}), f32[32,8,2048]{2,1,0:T(8,128)S(1)}, u32[]{:S(2)}, u32[]{:S(2)}) %all-to-all-start) | async-done | bytes 2097184 | tf_op jit(solution)/shard_map/all_to_all | solution.py:22
  253.5 0.8 broadcast_in_dim.9
  254.3 4.2 all-to-all-start.3
  258.5 0.1 reduce_sum.110
  258.6 10.5 %all-to-all-done.3 = f32[8,8,2048]{2,1,0:T(8,128)} async-done(((f32[8,8,2048]{2,1,0:T(8,128)}), f32[8,8,2048]{2,1,0:T(8,128)}, u32[]{:S(2)}, u32[]{:S(2)}) %all-to-all-start.3) | async-done | bytes 524320 | tf_op jit(solution)/shard_map/all_to_all | solution.py:28
  269.1 0.8 broadcast_in_dim.8
  269.9 3.5 all-to-all-start.1
  273.4 0.0 all-gather.16.cloned.1.call-start
  273.4 1.1 reduce_sum.113
  274.5 8.1 %all-to-all-done.1 = f32[8,8,2048]{2,1,0:T(8,128)S(1)} async-done(((f32[8,8,2048]{2,1,0:T(8,128)}), f32[8,8,2048]{2,1,0:T(8,128)S(1)}, u32[]{:S(2)}, u32[]{:S(2)}) %all-to-all-start.1) | async-done | bytes 524320 | tf_op jit(solution)/shard_map/all_to_all | solution.py:28
  282.7 2.8 fusion.96
  285.6 5.7 %fusion.12 = f32[2,4,2048]{2,1,0:T(4,128)S(1)} fusion(bf16[2,2048,512]{2,1,0:T(8,128)(2,1)} %param.7, f32[2,4,512]{2,1,0:T(4,128)S(1)} %fusion.96, bf16[2,4,2048]{2,1,0:T(4,128)(2,1)S(1)} %convert_element_type.52, bf16[2,512,2048]{2,1,0:T(8,128)(2,1)} %param.8), kind=kOutput, calls=%fused_computation.27 | convolution fusion | flops 33636352 | bytes 8503296 | tf_op jit(solution)/shard_map/esh,edh->esd/dot_general | solution.py:115
  291.3 0.1 broadcast_in_dim.10
  291.4 11.4 %all_to_all.40 = f32[8,2,4,2048]{3,2,1,0:T(4,128)S(1)} all-to-all(f32[8,2,4,2048]{3,2,1,0:T(4,128)S(1)} %broadcast_in_dim.10), channel_id=1, replica_groups=mesh['seq_0'=4,'seq_1'=2,'exp_0'=8,'exp_1'=2,'exp_2'=2] {'seq_0','seq_1'}, dimensions={0} | all-to-all | bytes 1048576 | tf_op jit(solution)/shard_map/all_to_all | solution.py:28
  302.8 0.1 reduce_sum.114
  302.9 0.6 convert_element_type.57
  303.5 0.0 all-gather.16.cloned.1.call-update
  303.6 0.0 copy-start.2
  303.6 0.0 all-gather.18.cloned.1.call-start
  303.6 2.9 fusion.14
  306.5 0.1 broadcast_in_dim.22
  306.7 11.6 %all_to_all.41 = f32[8,2,4,2048]{3,2,1,0:T(4,128)S(1)} all-to-all(f32[8,2,4,2048]{3,2,1,0:T(4,128)S(1)} %broadcast_in_dim.22), channel_id=1, replica_groups=mesh['seq_0'=4,'seq_1'=2,'exp_0'=8,'exp_1'=2,'exp_2'=2] {'seq_0','seq_1'}, dimensions={0} | all-to-all | bytes 1048576 | tf_op jit(solution)/shard_map/all_to_all | solution.py:28
  318.2 0.1 reduce_sum.116
  318.3 0.6 convert_element_type.61
  318.9 0.0 all-gather.18.cloned.1.call-update
  319.0 55.8 %all-gather.16.cloned.1.call-done = bf16[256,2048]{1,0:T(8,128)(2,1)} async-done(((bf16[8,2048]{1,0:T(8,128)(2,1)}), bf16[256,2048]{1,0:T(8,128)(2,1)}) %all-gather.16.cloned.1.call-update) | async-done | bytes 1048592 | tf_op jit(solution)/shard_map/all_gather | solution.py:117
  374.8 1.7 multiply_reduce_fusion.1
  376.5 0.0 copy-start.3
  376.5 10.5 %psum.35 = f32[256]{0:T(256)S(1)} all-reduce(f32[256]{0:T(256)S(1)} %get-tuple-element.23), channel_id=1, replica_groups=mesh['seq_0'=4,'seq_1'=2,'exp_0'=8,'exp_1'=2,'exp_2'=2] {'seq_0'}, use_global_device_ids=true, to_apply=%region_10.11 | all-reduce | flops 256 | bytes 2048 | tf_op jit(solution)/shard_map/psum | solution.py:62
  387.0 4.9 psum.36
  391.9 15.5 %psum.37 = f32[256]{0:T(256)S(1)} all-reduce(f32[256]{0:T(256)S(1)} %psum.36), channel_id=1, replica_groups=mesh['seq_0'=4,'seq_1'=2,'exp_0'=8,'exp_1'=2,'exp_2'=2] {'exp_0'}, use_global_device_ids=true, to_apply=%region_12.13 | all-reduce | flops 256 | bytes 2048 | tf_op jit(solution)/shard_map/psum | solution.py:62
  407.5 6.4 %psum.38 = f32[256]{0:T(256)S(1)} all-reduce(f32[256]{0:T(256)S(1)} %psum.37), channel_id=1, replica_groups=mesh['seq_0'=4,'seq_1'=2,'exp_0'=8,'exp_1'=2,'exp_2'=2] {'exp_1'}, use_global_device_ids=true, to_apply=%region_13.14 | all-reduce | flops 256 | bytes 2048 | tf_op jit(solution)/shard_map/psum | solution.py:62
  413.9 2.4 psum.39
  416.4 35.9 %all-gather.18.cloned.1.call-done = bf16[256,2048]{1,0:T(8,128)(2,1)} async-done(((bf16[8,2048]{1,0:T(8,128)(2,1)}), bf16[256,2048]{1,0:T(8,128)(2,1)}) %all-gather.18.cloned.1.call-update) | async-done | bytes 1048592 | tf_op jit(solution)/shard_map/all_gather | solution.py:108
  452.3 0.0 copy-done.2
  452.3 1.8 multiply_reduce_fusion
  454.1 1.9 convolution_bitcast_fusion
  456.0 7.6 %all-to-all-start.6 = ((f32[32,2048,8]{1,2,0:T(8,128)}), f32[32,2048,8]{1,2,0:T(8,128)S(1)}, u32[]{:S(2)}, u32[]{:S(2)}) async-start(f32[32,2048,8]{1,2,0:T(8,128)} %convolution_bitcast_fusion), calls=%async_computation.6 | async-start | bytes 4194304 | tf_op jit(solution)/shard_map/all_to_all | solution.py:22
  463.6 3.0 fusion.93
  466.6 47.1 %all-to-all-done.6 = f32[32,2048,8]{1,2,0:T(8,128)S(1)} async-done(((f32[32,2048,8]{1,2,0:T(8,128)}), f32[32,2048,8]{1,2,0:T(8,128)S(1)}, u32[]{:S(2)}, u32[]{:S(2)}) %all-to-all-start.6) | async-done | bytes 2097184 | tf_op jit(solution)/shard_map/all_to_all | solution.py:22
  513.8 0.7 reduce_sum.118
  514.5 4.9 all-to-all-start.7
  519.4 3.6 fusion
  523.0 2.8 all-to-all-done.7
  525.8 0.6 reduce_sum.119
  (18 shorter events, 0.2 us)
Async XLA Ops:
  7.2 82.5 %copy-start = (bf16[256,2048]{1,0:T(8,128)(2,1)S(1)}, bf16[256,2048]{1,0:T(8,128)(2,1)}, u32[]{:S(2)}) copy-start(bf16[256,2048]{1,0:T(8,128)(2,1)} %param.5) | copy-start | bytes 3145732
  7.2 82.5 %all-gather.14.cloned.1.call-start = ((), (), s32[]{:S(2)}) async-start(), calls=%async_computation.8 | async-start | bytes 1081344 | tf_op jit(solution)/shard_map/all_gather | solution.py:93
  138.4 57.3 %all-to-all-start.2 = ((f32[32,8,2048]{2,1,0:T(8,128)}), f32[32,8,2048]{2,1,0:T(8,128)S(1)}, u32[]{:S(2)}, u32[]{:S(2)}) async-start(f32[32,8,2048]{2,1,0:T(8,128)} %convolution_bitcast_fusion.1), calls=%async_computation.2 | async-start | bytes 4194304 | tf_op jit(solution)/shard_map/all_to_all | solution.py:22
  195.7 1.3 copy-start.1
  197.0 56.4 %all-to-all-start = ((f32[32,8,2048]{2,1,0:T(8,128)}), f32[32,8,2048]{2,1,0:T(8,128)S(1)}, u32[]{:S(2)}, u32[]{:S(2)}) async-start(f32[32,8,2048]{2,1,0:T(8,128)} %convolution_bitcast_fusion.2), calls=%async_computation | async-start | bytes 4194304 | tf_op jit(solution)/shard_map/all_to_all | solution.py:22
  254.3 14.8 %all-to-all-start.3 = ((f32[8,8,2048]{2,1,0:T(8,128)}), f32[8,8,2048]{2,1,0:T(8,128)}, u32[]{:S(2)}, u32[]{:S(2)}) async-start(f32[8,8,2048]{2,1,0:T(8,128)} %broadcast_in_dim.9), calls=%async_computation.3 | async-start | bytes 1048576 | tf_op jit(solution)/shard_map/all_to_all | solution.py:28
  269.9 12.8 %all-to-all-start.1 = ((f32[8,8,2048]{2,1,0:T(8,128)}), f32[8,8,2048]{2,1,0:T(8,128)S(1)}, u32[]{:S(2)}, u32[]{:S(2)}) async-start(f32[8,8,2048]{2,1,0:T(8,128)} %broadcast_in_dim.8), calls=%async_computation.1 | async-start | bytes 1048576 | tf_op jit(solution)/shard_map/all_to_all | solution.py:28
  273.4 101.4 %all-gather.16.cloned.1.call-start = ((), (), s32[]{:S(2)}) async-start(), calls=%async_computation.9 | async-start | bytes 1081344 | tf_op jit(solution)/shard_map/all_gather | solution.py:117
  303.6 148.7 %copy-start.2 = (bf16[256,2048]{1,0:T(8,128)(2,1)S(1)}, bf16[256,2048]{1,0:T(8,128)(2,1)}, u32[]{:S(2)}) copy-start(bf16[256,2048]{1,0:T(8,128)(2,1)} %param.9) | copy-start | bytes 3145732
  303.6 148.7 %all-gather.18.cloned.1.call-start = ((), (), s32[]{:S(2)}) async-start(), calls=%async_computation.10 | async-start | bytes 1081344 | tf_op jit(solution)/shard_map/all_gather | solution.py:108
  376.5 79.5 %copy-start.3 = (f32[256,256]{1,0:T(8,128)}, f32[256,256]{1,0:T(8,128)S(1)}, u32[]{:S(2)}) copy-start(f32[256,256]{1,0:T(8,128)S(1)} %get-tuple-element.24) | copy-start | bytes 786436
  454.1 1.9 copy-start.4
  456.0 57.7 %all-to-all-start.6 = ((f32[32,2048,8]{1,2,0:T(8,128)}), f32[32,2048,8]{1,2,0:T(8,128)S(1)}, u32[]{:S(2)}, u32[]{:S(2)}) async-start(f32[32,2048,8]{1,2,0:T(8,128)} %convolution_bitcast_fusion), calls=%async_computation.6 | async-start | bytes 4194304 | tf_op jit(solution)/shard_map/all_to_all | solution.py:22
  514.5 11.3 %all-to-all-start.7 = ((f32[8,256,8]{1,2,0:T(8,128)}), f32[8,256,8]{1,2,0:T(8,128)S(1)}, u32[]{:S(2)}, u32[]{:S(2)}) async-start(f32[8,256,8]{1,2,0:T(8,128)} %bitcast.50), calls=%async_computation.7 | async-start | bytes 131072 | tf_op jit(solution)/shard_map/all_to_all | solution.py:22
Sparse Core Ops, SparseCore 0:
  10.8 78.8 all-gather.13
  303.7 71.0 all-gather.15
  377.6 74.6 all-gather.17
where the time goes:
time: 534 us; the launch traced here: 533 us
  waiting for transfers between devices  338 us (63%)
  blocking collectives  108 us (20%)
  starting transfers between devices  33.7 us (6%)
  matrix products  30.2 us (6%)
  between operations  13.9 us (3%)
    all_to_all x4, waiting for transfers between devices, sum_at_owner(): blocks = lax.all_to_all(split_up(x, dim, size), axis, 0, 0, tiled=True)  145 us
    all_gather x1, waiting for transfers between devices, shards(): slot_table = lax.all_gather(slot_embed, EXP, axis=1, tiled=True)  81.8 us
    all_gather x1, waiting for transfers between devices, shards(): grad_all = lax.all_gather(grad_own, EXP, axis=0, tiled=True)  55.8 us
    all_gather x5, blocking collectives, collected_together(): both, at, found = (lax.all_gather(jnp.concatenate(lines), axis), 0, {})  44.8 us
    psum x5, blocking collectives, one_axis_at_a_time(): return functools.reduce(lax.psum, axes, x)  39.9 us
    all_gather x1, waiting for transfers between devices, shards(): slot_all = lax.all_gather(slot_out, EXP, axis=0, tiled=True)  35.9 us
    all_to_all x4, starting transfers between devices, sum_at_owner(): blocks = lax.all_to_all(split_up(x, dim, size), axis, 0, 0, tiled=True)  25.9 us
    all_to_all x2, blocking collectives, from_everyone(): return lax.all_to_all(copies, axis, split_axis=0, concat_axis=0, tiled=True)  23 us
  transfers between devices with their start and end apart: 9, of which 9 were waited for; matrix products, arithmetic and copies ran while one was open for 3% of the time, Pallas kernels for 0%

commit v1 on v0

--- a/solution.py
+++ b/solution.py
@@ -105,7 +105,9 @@
     hidden = jax.nn.gelu(pre_act, approximate=True).astype(jnp.bfloat16)
     out_part = jnp.einsum("esh,ehd->esd", hidden, expert_out, preferred_element_type=jnp.float32)
     slot_out = taken_together(out_part, SEQ).astype(jnp.bfloat16).reshape(-1, model_width)
-    slot_all = lax.all_gather(slot_out, EXP, axis=0, tiled=True)
+    slot_all = jnp.concatenate(
+        lax.all_to_all(jnp.stack([slot_out] * lax.axis_size(EXP)), EXP, 0, 0), axis=0
+    )
     comb_grad = contract_cols(out_grad, slot_all)
     grad_out = owner_sum(contract_rows(combine_b, out_grad))
     grad_out = grad_out.astype(jnp.bfloat16).reshape(experts_here, -1, model_width)

time: 534 us -> 512 us (0.959)
  blocking collectives: 108 us -> 84.6 us
  waiting for transfers between devices: 338 us -> 323 us
  starting transfers between devices: 33.7 us -> 46.2 us
    all_gather x1 -> x0, waiting for transfers between devices: 35.9 us -> none  [shards(): slot_all = lax.all_gather(slot_out, EXP, axis=0, tiled=True)]
    all_to_all x2 -> x0, blocking collectives: 23 us -> none  [from_everyone(): return lax.all_to_all(copies, axis, split_axis=0, concat_axis=0, tiled=True)]
    all_to_all x2 -> x4, waiting for transfers between devices: 18.6 us -> 32.4 us  [from_everyone(): return lax.all_to_all(copies, axis, split_axis=0, concat_axis=0, tiled=True)]
    all_to_all x2 -> x4, starting transfers between devices: 7.65 us -> 14.8 us  [from_everyone(): return lax.all_to_all(copies, axis, split_axis=0, concat_axis=0, tiled=True)]
    all_gather x1, waiting for transfers between devices: 55.8 us -> 62.5 us  [shards(): grad_all = lax.all_gather(grad_own, EXP, axis=0, tiled=True)]
    all_to_all x0 -> x1, starting transfers between devices: none -> 5.99 us  [shards(): lax.all_to_all(jnp.stack([slot_out] * lax.axis_size(EXP)), EXP, 0, 0)]
  transfers between devices with their start and end apart: 9 -> 11, of which waited for: 9 -> 10; matrix products, arithmetic and copies ran while one was open for 3% -> 4% of each run, Pallas kernels for 0% -> 0%
where the time goes in v1:
time: 512 us; the launch traced here: 510 us
  waiting for transfers between devices  323 us (63%)
  blocking collectives  84.6 us (17%)
  starting transfers between devices  46.2 us (9%)
  matrix products  30.6 us (6%)
  between operations  14.2 us (3%)
  local copies, waits for them, and re-layouts  7.24 us (1%)
    all_to_all x4, waiting for transfers between devices, sum_at_owner(): blocks = lax.all_to_all(split_up(x, dim, size), axis, 0, 0, tiled=True)  145 us
    all_gather x1, waiting for transfers between devices, shards(): slot_table = lax.all_gather(slot_embed, EXP, axis=1, tiled=True)  81.8 us
    all_gather x1, waiting for transfers between devices, shards(): grad_all = lax.all_gather(grad_own, EXP, axis=0, tiled=True)  62.5 us
    all_gather x5, blocking collectives, collected_together(): both, at, found = (lax.all_gather(jnp.concatenate(lines), axis), 0, {})  44.8 us
    psum x5, blocking collectives, one_axis_at_a_time(): return functools.reduce(lax.psum, axes, x)  39.8 us
    all_to_all x4, waiting for transfers between devices, from_everyone(): return lax.all_to_all(copies, axis, split_axis=0, concat_axis=0, tiled=True)  32.4 us
    all_to_all x4, starting transfers between devices, sum_at_owner(): blocks = lax.all_to_all(split_up(x, dim, size), axis, 0, 0, tiled=True)  25.4 us
    all_to_all x4, starting transfers between devices, from_everyone(): return lax.all_to_all(copies, axis, split_axis=0, concat_axis=0, tiled=True)  14.8 us
  transfers between devices with their start and end apart: 11, of which 10 were waited for; matrix products, arithmetic and copies ran while one was open for 4% of the time, Pallas kernels for 0%

profile of v1, /device:TPU:4, one launch (start us, length us, event | category | flops | bytes accessed | tf_op | source)
XLA Modules:
  0.0 510.2 jit_solution(1346751070956218530)
XLA Ops:
  7.2 0.0 copy-start
  7.2 0.0 all-gather.13.cloned.1.call-start
  7.2 0.7 all-gather.13.cloned.1.call-update
  7.9 81.8 %all-gather.13.cloned.1.call-done = bf16[2048,256]{0,1:T(8,128)(2,1)} async-done(((bf16[2048,8]{0,1:T(8,128)(2,1)}), bf16[2048,256]{0,1:T(8,128)(2,1)}) %all-gather.13.cloned.1.call-update) | async-done | bytes 1048592 | tf_op jit(solution)/shard_map/all_gather | solution.py:93
  89.7 0.0 copy-done
  89.7 1.8 fusion.86
  91.5 0.2 fusion.3
  91.7 11.2 %all-gather.5 = f32[4,2,256]{2,1,0:T(2,128)S(1)} all-gather(f32[1,2,256]{2,1,0:T(2,128)S(1)} %maximum_bitcast_fusion), channel_id=2, replica_groups=mesh['seq_0'=4,'seq_1'=2,'exp_0'=8,'exp_1'=2,'exp_2'=2] {'seq_0'}, dimensions={0}, use_global_device_ids=true | all-gather | bytes 10240 | tf_op jit(solution)/shard_map/all_gather | solution.py:43
  102.9 4.4 all-gather.6
  107.3 21.6 %all-gather.7 = f32[8,2,256]{2,1,0:T(2,128)S(1)} all-gather(f32[1,2,256]{2,1,0:T(2,128)S(1)} %maximum_bitcast_fusion.2), channel_id=4, replica_groups=mesh['seq_0'=4,'seq_1'=2,'exp_0'=8,'exp_1'=2,'exp_2'=2] {'exp_0'}, dimensions={0}, use_global_device_ids=true | all-gather | bytes 18432 | tf_op jit(solution)/shard_map/all_gather | solution.py:43
  128.9 5.9 %all-gather.8 = f32[2,2,256]{2,1,0:T(2,128)S(1)} all-gather(f32[1,2,256]{2,1,0:T(2,128)S(1)} %maximum_bitcast_fusion.3), channel_id=5, replica_groups=mesh['seq_0'=4,'seq_1'=2,'exp_0'=8,'exp_1'=2,'exp_2'=2] {'exp_1'}, dimensions={0}, use_global_device_ids=true | all-gather | bytes 6144 | tf_op jit(solution)/shard_map/all_gather | solution.py:43
  134.8 1.8 all-gather.9
  136.7 1.8 convolution_bitcast_fusion.1
  138.4 7.1 %all-to-all-start.2 = ((f32[32,8,2048]{2,1,0:T(8,128)}), f32[32,8,2048]{2,1,0:T(8,128)S(1)}, u32[]{:S(2)}, u32[]{:S(2)}) async-start(f32[32,8,2048]{2,1,0:T(8,128)} %convolution_bitcast_fusion.1), calls=%async_computation.2 | async-start | bytes 4194304 | tf_op jit(solution)/shard_map/all_to_all | solution.py:22
  145.6 3.2 convolution_bitcast_fusion.2
  148.7 47.0 %all-to-all-done.2 = f32[32,8,2048]{2,1,0:T(8,128)S(1)} async-done(((f32[32,8,2048]{2,1,0:T(8,128)}), f32[32,8,2048]{2,1,0:T(8,128)S(1)}, u32[]{:S(2)}, u32[]{:S(2)}) %all-to-all-start.2) | async-done | bytes 2097184 | tf_op jit(solution)/shard_map/all_to_all | solution.py:22
  195.7 1.3 copy-done.1
  197.0 6.3 %all-to-all-start = ((f32[32,8,2048]{2,1,0:T(8,128)}), f32[32,8,2048]{2,1,0:T(8,128)S(1)}, u32[]{:S(2)}, u32[]{:S(2)}) async-start(f32[32,8,2048]{2,1,0:T(8,128)} %convolution_bitcast_fusion.2), calls=%async_computation | async-start | bytes 4194304 | tf_op jit(solution)/shard_map/all_to_all | solution.py:22
  203.3 1.7 reduce_sum.112
  205.0 48.5 %all-to-all-done = f32[32,8,2048]{2,1,0:T(8,128)S(1)} async-done(((f32[32,8,2048]{2,1,0:T(8,128)}), f32[32,8,2048]{2,1,0:T(8,128)S(1)}, u32[]{:S(2)}, u32[]{:S(2)}) %all-to-all-start) | async-done | bytes 2097184 | tf_op jit(solution)/shard_map/all_to_all | solution.py:22
  253.5 0.8 broadcast_in_dim.9
  254.3 4.2 all-to-all-start.3
  258.5 0.1 reduce_sum.110
  258.6 10.5 %all-to-all-done.3 = f32[8,8,2048]{2,1,0:T(8,128)} async-done(((f32[8,8,2048]{2,1,0:T(8,128)}), f32[8,8,2048]{2,1,0:T(8,128)}, u32[]{:S(2)}, u32[]{:S(2)}) %all-to-all-start.3) | async-done | bytes 524320 | tf_op jit(solution)/shard_map/all_to_all | solution.py:28
  269.1 0.8 broadcast_in_dim.8
  269.9 3.5 all-to-all-start.1
  273.4 1.1 reduce_sum.113
  274.5 8.2 %all-to-all-done.1 = f32[8,8,2048]{2,1,0:T(8,128)S(1)} async-done(((f32[8,8,2048]{2,1,0:T(8,128)}), f32[8,8,2048]{2,1,0:T(8,128)S(1)}, u32[]{:S(2)}, u32[]{:S(2)}) %all-to-all-start.1) | async-done | bytes 524320 | tf_op jit(solution)/shard_map/all_to_all | solution.py:28
  282.7 2.8 fusion.97
  285.6 5.7 %fusion.13 = f32[2,4,2048]{2,1,0:T(4,128)S(1)} fusion(bf16[2,2048,512]{2,1,0:T(8,128)(2,1)} %param.7, f32[2,4,512]{2,1,0:T(4,128)S(1)} %fusion.97, bf16[2,4,2048]{2,1,0:T(4,128)(2,1)S(1)} %convert_element_type.53, bf16[2,512,2048]{2,1,0:T(8,128)(2,1)} %param.8), kind=kOutput, calls=%fused_computation.28 | convolution fusion | flops 33636352 | bytes 8503296 | tf_op jit(solution)/shard_map/esh,edh->esd/dot_general | solution.py:117
  291.3 0.9 broadcast_in_dim.10
  292.2 3.5 all-to-all-start.4
  295.7 2.8 fusion.15
  298.6 5.9 %all-to-all-done.4 = f32[8,2,4,2048]{3,2,1,0:T(4,128)S(1)} async-done(((f32[8,2,4,2048]{3,2,1,0:T(4,128)}), f32[8,2,4,2048]{3,2,1,0:T(4,128)S(1)}, u32[]{:S(2)}, u32[]{:S(2)}) %all-to-all-start.4) | async-done | bytes 524320 | tf_op jit(solution)/shard_map/all_to_all | solution.py:28
  304.4 0.9 broadcast_in_dim.22
  305.3 3.6 all-to-all-start.5
  308.9 0.0 all-gather.15.cloned.1.call-start
  309.0 0.1 reduce_sum.114
  309.1 0.6 convert_element_type.58
  309.7 0.0 all-gather.15.cloned.1.call-update
  309.7 7.8 %all-to-all-done.5 = f32[8,2,4,2048]{3,2,1,0:T(4,128)S(1)} async-done(((f32[8,2,4,2048]{3,2,1,0:T(4,128)}), f32[8,2,4,2048]{3,2,1,0:T(4,128)S(1)}, u32[]{:S(2)}, u32[]{:S(2)}) %all-to-all-start.5) | async-done | bytes 524320 | tf_op jit(solution)/shard_map/all_to_all | solution.py:28
  317.6 0.1 reduce_sum.116
  317.7 1.1 stack.3
  318.8 6.0 %all-to-all-start.6 = ((bf16[32,8,2048]{2,1,0:T(8,128)(2,1)}), bf16[32,8,2048]{2,1,0:T(8,128)(2,1)S(1)}, u32[]{:S(2)}, u32[]{:S(2)}) async-start(bf16[32,8,2048]{2,1,0:T(8,128)(2,1)} %stack.3), calls=%async_computation.6 | async-start | bytes 2097152 | tf_op jit(solution)/shard_map/all_to_all | solution.py:109
  324.8 62.5 %all-gather.15.cloned.1.call-done = bf16[256,2048]{1,0:T(8,128)(2,1)} async-done(((bf16[8,2048]{1,0:T(8,128)(2,1)}), bf16[256,2048]{1,0:T(8,128)(2,1)}) %all-gather.15.cloned.1.call-update) | async-done | bytes 1048592 | tf_op jit(solution)/shard_map/all_gather | solution.py:119
  387.3 2.4 multiply_reduce_fusion.1
  389.7 10.4 %psum.35 = f32[256]{0:T(256)S(1)} all-reduce(f32[256]{0:T(256)S(1)} %get-tuple-element.23), channel_id=1, replica_groups=mesh['seq_0'=4,'seq_1'=2,'exp_0'=8,'exp_1'=2,'exp_2'=2] {'seq_0'}, use_global_device_ids=true, to_apply=%region_10.11 | all-reduce | flops 256 | bytes 2048 | tf_op jit(solution)/shard_map/psum | solution.py:62
  400.1 4.9 psum.36
  405.0 15.6 %psum.37 = f32[256]{0:T(256)S(1)} all-reduce(f32[256]{0:T(256)S(1)} %psum.36), channel_id=1, replica_groups=mesh['seq_0'=4,'seq_1'=2,'exp_0'=8,'exp_1'=2,'exp_2'=2] {'exp_0'}, use_global_device_ids=true, to_apply=%region_12.13 | all-reduce | flops 256 | bytes 2048 | tf_op jit(solution)/shard_map/psum | solution.py:62
  420.6 6.4 %psum.38 = f32[256]{0:T(256)S(1)} all-reduce(f32[256]{0:T(256)S(1)} %psum.37), channel_id=1, replica_groups=mesh['seq_0'=4,'seq_1'=2,'exp_0'=8,'exp_1'=2,'exp_2'=2] {'exp_1'}, use_global_device_ids=true, to_apply=%region_13.14 | all-reduce | flops 256 | bytes 2048 | tf_op jit(solution)/shard_map/psum | solution.py:62
  427.0 2.4 psum.39
  429.5 0.0 all-to-all-done.6
  429.5 0.0 copy-done.2
  429.5 0.6 multiply_reduce_fusion
  430.0 0.7 copy-done.3
  430.7 2.9 convolution_bitcast_fusion
  433.6 8.6 %all-to-all-start.7 = ((f32[32,2048,8]{1,2,0:T(8,128)}), f32[32,2048,8]{1,2,0:T(8,128)S(1)}, u32[]{:S(2)}, u32[]{:S(2)}) async-start(f32[32,2048,8]{1,2,0:T(8,128)} %convolution_bitcast_fusion), calls=%async_computation.7 | async-start | bytes 4194304 | tf_op jit(solution)/shard_map/all_to_all | solution.py:22
  442.2 3.0 fusion.94
  445.2 47.1 %all-to-all-done.7 = f32[32,2048,8]{1,2,0:T(8,128)S(1)} async-done(((f32[32,2048,8]{1,2,0:T(8,128)}), f32[32,2048,8]{1,2,0:T(8,128)S(1)}, u32[]{:S(2)}, u32[]{:S(2)}) %all-to-all-start.7) | async-done | bytes 2097184 | tf_op jit(solution)/shard_map/all_to_all | solution.py:22
  492.4 0.7 reduce_sum.118
  493.1 3.3 all-to-all-start.8
  496.5 3.6 fusion
  500.1 2.7 all-to-all-done.8
  502.7 0.6 reduce_sum.119
  (18 shorter events, 0.2 us)
Async XLA Ops:
  7.2 82.5 %copy-start = (bf16[256,2048]{1,0:T(8,128)(2,1)S(1)}, bf16[256,2048]{1,0:T(8,128)(2,1)}, u32[]{:S(2)}) copy-start(bf16[256,2048]{1,0:T(8,128)(2,1)} %param.5) | copy-start | bytes 3145732
  7.2 82.5 %all-gather.13.cloned.1.call-start = ((), (), s32[]{:S(2)}) async-start(), calls=%async_computation.9 | async-start | bytes 1081344 | tf_op jit(solution)/shard_map/all_gather | solution.py:93
  138.4 57.3 %all-to-all-start.2 = ((f32[32,8,2048]{2,1,0:T(8,128)}), f32[32,8,2048]{2,1,0:T(8,128)S(1)}, u32[]{:S(2)}, u32[]{:S(2)}) async-start(f32[32,8,2048]{2,1,0:T(8,128)} %convolution_bitcast_fusion.1), calls=%async_computation.2 | async-start | bytes 4194304 | tf_op jit(solution)/shard_map/all_to_all | solution.py:22
  195.7 1.3 copy-start.1
  197.0 56.4 %all-to-all-start = ((f32[32,8,2048]{2,1,0:T(8,128)}), f32[32,8,2048]{2,1,0:T(8,128)S(1)}, u32[]{:S(2)}, u32[]{:S(2)}) async-start(f32[32,8,2048]{2,1,0:T(8,128)} %convolution_bitcast_fusion.2), calls=%async_computation | async-start | bytes 4194304 | tf_op jit(solution)/shard_map/all_to_all | solution.py:22
  254.3 14.8 %all-to-all-start.3 = ((f32[8,8,2048]{2,1,0:T(8,128)}), f32[8,8,2048]{2,1,0:T(8,128)}, u32[]{:S(2)}, u32[]{:S(2)}) async-start(f32[8,8,2048]{2,1,0:T(8,128)} %broadcast_in_dim.9), calls=%async_computation.3 | async-start | bytes 1048576 | tf_op jit(solution)/shard_map/all_to_all | solution.py:28
  269.9 12.8 %all-to-all-start.1 = ((f32[8,8,2048]{2,1,0:T(8,128)}), f32[8,8,2048]{2,1,0:T(8,128)S(1)}, u32[]{:S(2)}, u32[]{:S(2)}) async-start(f32[8,8,2048]{2,1,0:T(8,128)} %broadcast_in_dim.8), calls=%async_computation.1 | async-start | bytes 1048576 | tf_op jit(solution)/shard_map/all_to_all | solution.py:28
  292.2 12.2 %all-to-all-start.4 = ((f32[8,2,4,2048]{3,2,1,0:T(4,128)}), f32[8,2,4,2048]{3,2,1,0:T(4,128)S(1)}, u32[]{:S(2)}, u32[]{:S(2)}) async-start(f32[8,2,4,2048]{3,2,1,0:T(4,128)} %broadcast_in_dim.10), calls=%async_computation.4 | async-start | bytes 1048576 | tf_op jit(solution)/shard_map/all_to_all | solution.py:28
  305.3 124.2 %copy-start.2 = (bf16[256,2048]{1,0:T(8,128)(2,1)S(1)}, bf16[256,2048]{1,0:T(8,128)(2,1)}, u32[]{:S(2)}) copy-start(bf16[256,2048]{1,0:T(8,128)(2,1)} %param.9) | copy-start | bytes 3145732
  305.3 12.3 %all-to-all-start.5 = ((f32[8,2,4,2048]{3,2,1,0:T(4,128)}), f32[8,2,4,2048]{3,2,1,0:T(4,128)S(1)}, u32[]{:S(2)}, u32[]{:S(2)}) async-start(f32[8,2,4,2048]{3,2,1,0:T(4,128)} %broadcast_in_dim.22), calls=%async_computation.5 | async-start | bytes 1048576 | tf_op jit(solution)/shard_map/all_to_all | solution.py:28
  308.9 78.3 %all-gather.15.cloned.1.call-start = ((), (), s32[]{:S(2)}) async-start(), calls=%async_computation.10 | async-start | bytes 1081344 | tf_op jit(solution)/shard_map/all_gather | solution.py:119
  318.8 110.7 %all-to-all-start.6 = ((bf16[32,8,2048]{2,1,0:T(8,128)(2,1)}), bf16[32,8,2048]{2,1,0:T(8,128)(2,1)S(1)}, u32[]{:S(2)}, u32[]{:S(2)}) async-start(bf16[32,8,2048]{2,1,0:T(8,128)(2,1)} %stack.3), calls=%async_computation.6 | async-start | bytes 2097152 | tf_op jit(solution)/shard_map/all_to_all | solution.py:109
  430.0 0.7 copy-start.3
  433.6 58.8 %all-to-all-start.7 = ((f32[32,2048,8]{1,2,0:T(8,128)}), f32[32,2048,8]{1,2,0:T(8,128)S(1)}, u32[]{:S(2)}, u32[]{:S(2)}) async-start(f32[32,2048,8]{1,2,0:T(8,128)} %convolution_bitcast_fusion), calls=%async_computation.7 | async-start | bytes 4194304 | tf_op jit(solution)/shard_map/all_to_all | solution.py:22
  493.1 9.6 %all-to-all-start.8 = ((f32[8,256,8]{1,2,0:T(8,128)}), f32[8,256,8]{1,2,0:T(8,128)S(1)}, u32[]{:S(2)}, u32[]{:S(2)}) async-start(f32[8,256,8]{1,2,0:T(8,128)} %bitcast.51), calls=%async_computation.8 | async-start | bytes 131072 | tf_op jit(solution)/shard_map/all_to_all | solution.py:22
Sparse Core Ops, SparseCore 0:
  10.8 78.8 all-gather.12
  312.5 74.6 all-gather.14
